TPU v7x, 32 devices: a whole 2x2x4 slice. The times are simulated.
32 devices in a mesh: gx: 4 (over z), gy: 4 (over y, x), gz: 2 (over core).
Axes of the slice: x: 2, y: 2, z: 4, core: 2. Of those that a mesh axis runs over, the one named last changes fastest.
Arguments:
- pair: bfloat16 [128, 128, 128], P('gx', ('gy', 'gz')), may hold values from -6 to 6
- pair_mask: int32 [128, 128], P('gx', ('gy', 'gz')), may hold values 0 or 1
- in_gain: float32 [128], replicated, may hold values from 0.1 to 1.9
- in_bias: float32 [128], replicated, may hold values from -3 to 3
- proj_weight: bfloat16 [128, 512], replicated, may hold values from -0.5 to 0.5
- gate_weight: bfloat16 [128, 128], replicated, may hold values from -0.5 to 0.5
- out_gain: float32 [128], replicated, may hold values from 0.1 to 1.9
- out_bias: float32 [128], replicated, may hold values from -3 to 3
- out_weight: bfloat16 [128, 128], replicated, may hold values from -0.5 to 0.5
Outputs:
- update: bfloat16 [128, 128, 128], P('gx', ('gy', 'gz'))
All inputs are finite; a program needn't handle non-finite values. No bound on the sum of `pair_mask` on one device may be relied on, other than what follows from the above.
Results may differ from a plain program's by a relative error of at most 0.0071.
Values may be sent and summed in bfloat16 or wider, within the bound.
A program may use at most 64 MiB of HBM per device.

v0:
```python
import jax
import jax.numpy as jnp
from jax import lax
from jax.sharding import PartitionSpec as P


def normalize(values, gain, bias):
    average = jnp.mean(values, axis=-1, keepdims=True)
    centered = values - average
    variance = jnp.mean(centered * centered, axis=-1, keepdims=True)
    return centered * lax.rsqrt(variance + 1e-05) * gain + bias


def project(tile, mask_value, in_gain, in_bias, proj_weight):
    hidden = proj_weight.shape[1] // 4
    normed = normalize(tile.astype(jnp.float32), in_gain, in_bias).astype(jnp.bfloat16)
    projected = jnp.einsum("rwc,cd->rwd", normed, proj_weight, preferred_element_type=jnp.float32)
    left_side = (
        jax.nn.sigmoid(projected[:, :, :hidden]) * projected[:, :, hidden : 2 * hidden] * mask_value
    ).astype(jnp.bfloat16)
    right_side = (
        jax.nn.sigmoid(projected[:, :, 2 * hidden : 3 * hidden])
        * projected[:, :, 3 * hidden :]
        * mask_value
    ).astype(jnp.bfloat16)
    return (normed, left_side, right_side)


def on_device(
    pair, pair_mask, in_gain, in_bias, proj_weight, gate_weight, out_gain, out_bias, out_weight
):
    mask_value = pair_mask.astype(jnp.float32)[:, :, None]
    normed, left_side, own_right = project(pair, mask_value, in_gain, in_bias, proj_weight)
    left_slab, right_slab = (
        lax.all_gather(left_side, "gy", axis=1, tiled=True),
        lax.all_gather(own_right, "gy", axis=1, tiled=True),
    )
    every_row = lax.all_gather(own_right, "gx", axis=0, tiled=True)
    row_panel = lax.all_to_all(every_row, "gy", split_axis=0, concat_axis=1, tiled=True)
    summed = lax.psum_scatter(
        jnp.einsum("jkc,ikc->jic", row_panel, left_slab, preferred_element_type=jnp.float32),
        "gz",
        scatter_dimension=0,
        tiled=True,
    )
    triangle = jnp.transpose(summed, (1, 0, 2))
    tri_normed = normalize(triangle, out_gain, out_bias).astype(jnp.bfloat16)
    gating = jax.nn.sigmoid(
        jnp.einsum("rwc,cd->rwd", normed, gate_weight, preferred_element_type=jnp.float32)
    )
    mixed = jnp.einsum("rwh,hc->rwc", tri_normed, out_weight, preferred_element_type=jnp.float32)
    return (gating * mixed).astype(jnp.bfloat16)


def solution(mesh):
    return jax.shard_map(
        on_device,
        mesh=mesh,
        in_specs=(
            P("gx", ("gy", "gz"), None),
            P("gx", ("gy", "gz")),
            P(),
            P(),
            P(),
            P(),
            P(),
            P(),
            P(),
        ),
        out_specs=P("gx", ("gy", "gz"), None),
        check_vma=False,
    )
```

profile of v0, /device:TPU:0, one launch (start us, length us, event | category | flops | bytes accessed | tf_op | source)
XLA Modules:
  0.0 80.6 jit_solution(6983659560410940790)
XLA Ops:
  6.5 1.1 %convert_reduce_fusion = f32[32,16]{1,0:T(8,128)S(1)} fusion(bf16[32,16,128]{2,1,0:T(8,128)(2,1)} %param.9), kind=kLoop, calls=%fused_computation.8 | loop fusion | flops 130560 | bytes 133120 | tf_op jit(solution)/shard_map/reduce_sum | solution.py:8
  7.6 0.1 copy.52
  7.7 0.1 copy.53
  7.8 1.1 %fusion.6 = f32[32,16]{1,0:T(8,128)S(1)} fusion(bf16[32,16,128]{2,1,0:T(8,128)(2,1)} %param.9, f32[32,16]{1,0:T(8,128)S(1)} %copy.53), kind=kLoop, calls=%fused_computation.11 | loop fusion | flops 261632 | bytes 135168 | tf_op jit(solution)/shard_map/reduce_sum | solution.py:10
  8.9 0.1 copy.54
  9.0 0.1 copy.55
  9.1 0.7 convert_element_type.23
  9.8 0.1 copy.56
  9.9 1.3 %fusion.20 = f32[32,16,512]{2,1,0:T(8,128)S(1)} fusion(bf16[128,512]{1,0:T(8,128)(2,1)S(1)} %copy-done, bf16[32,16,128]{2,1,0:T(8,128)(2,1)} %param.9, f32[128]{0:T(128)} %param.12, f32[128]{0:T(128)} %param.11, f32[32,16]{1,0:T(8,128)S(1)} %copy.55, f32[32,16]{1,0:T(8,128)S(1)} %copy.53), kind=kOutput, calls=%fused_computation.33 | convolution fusion | flops 67502080 | bytes 1315840 | tf_op jit(solution)/shard_map/rwc,cd->rwd/dot_general | solution.py:17
  11.2 0.2 fusion.11
  11.3 18.0 %all_gather.7 = bf16[128,16,128]{2,1,0:T(8,128)(2,1)} all-gather(bf16[32,16,128]{2,1,0:T(8,128)(2,1)S(1)} %get-tuple-element.5), channel_id=1, replica_groups=mesh['gx'=4,'gy'=4,'gz'=2] {'gx'}, dimensions={0}, use_global_device_ids=true | all-gather | bytes 655360 | tf_op jit(solution)/shard_map/all_gather | solution.py:38
  29.3 3.7 %all-to-all-start = ((bf16[128,16,128]{2,1,0:T(8,128)(2,1)}), bf16[128,16,128]{2,1,0:T(8,128)(2,1)S(1)}, u32[]{:S(2)}, u32[]{:S(2)}) async-start(bf16[128,16,128]{2,1,0:T(8,128)(2,1)} %all_gather.7), calls=%async_computation | async-start | bytes 1048576 | tf_op jit(solution)/shard_map/all_to_all | solution.py:39
  33.1 15.6 %all_gather.6 = bf16[32,64,128]{2,1,0:T(8,128)(2,1)S(1)} all-gather(bf16[32,16,128]{2,1,0:T(8,128)(2,1)S(1)} %get-tuple-element.6), channel_id=1, replica_groups=mesh['gx'=4,'gy'=4,'gz'=2] {'gy'}, dimensions={1}, use_global_device_ids=true | all-gather | bytes 655360 | tf_op jit(solution)/shard_map/all_gather | solution.py:35
  48.7 3.2 %copy.58 = bf16[32,64,128]{0,1,2:T(8,128)(2,1)S(1)} copy(bf16[32,64,128]{2,1,0:T(8,128)(2,1)S(1)} %all_gather.6) | data formatting | bytes 1048576 | tf_op jit(solution)/shard_map/all_gather | solution.py:35
  51.9 0.9 %copy.57 = bf16[32,4,16,128]{3,2,1,0:T(8,128)(2,1)} copy(bf16[32,4,16,128]{3,2,0,1:T(8,128)(2,1)S(1)} %bitcast.25) | data formatting | bytes 1048576 | tf_op jit(solution)/shard_map/all_to_all | solution.py:39
  52.8 2.5 %copy.59 = bf16[32,64,128]{1,0,2:T(8,128)(2,1)S(1)} copy(bf16[32,64,128]{2,1,0:T(8,128)(2,1)} %bitcast.24) | data formatting | bytes 1048576 | tf_op jit(solution)/shard_map/all_to_all | solution.py:39
  55.2 2.1 %convolution_bitcast_fusion = f32[32,32,128]{0,1,2:T(8,128)} fusion(bf16[32,64,128]{0,1,2:T(8,128)(2,1)S(1)} %copy.58, bf16[32,64,128]{1,0,2:T(8,128)(2,1)S(1)} %copy.59), kind=kOutput, calls=%fused_computation | convolution fusion | flops 16777216 | bytes 1572864 | tf_op jit(solution)/shard_map/jkc,ikc->jic/dot_general | solution.py:41
  57.4 3.7 %copy.60 = f32[32,32,128]{2,1,0:T(8,128)} copy(f32[32,32,128]{0,1,2:T(8,128)} %convolution_bitcast_fusion) | data formatting | bytes 1048576 | tf_op jit(solution)/shard_map/jkc,ikc->jic/transpose | solution.py:41
  61.1 0.3 fusion.2
  61.5 7.9 %reduce-scatter.2.cloned.1.call-done = f32[16,32,128]{2,1,0:T(8,128)} async-done(((f32[32,32,128]{2,1,0:T(8,128)}), f32[16,32,128]{2,1,0:T(8,128)}) %reduce-scatter.2.cloned.1.call-update) | async-done | bytes 262160 | tf_op jit(solution)/shard_map/reduce_scatter | solution.py:40
  69.4 1.1 %bitcast_reduce_fusion = f32[32,16]{0,1:T(8,128)S(1)} fusion(f32[16,32,128]{2,1,0:T(8,128)} %reduce-scatter.2.cloned.1.call-done), kind=kLoop, calls=%fused_computation.30 | loop fusion | flops 65024 | bytes 264192 | tf_op jit(solution)/shard_map/reduce_sum | solution.py:8
  70.5 1.2 %multiply_reduce_fusion = f32[32,16]{0,1:T(8,128)S(1)} fusion(f32[16,32,128]{2,1,0:T(8,128)} %reduce-scatter.2.cloned.1.call-done, f32[32,16]{0,1:T(8,128)S(1)} %broadcast_multiply_fusion), kind=kLoop, calls=%fused_computation.32 | loop fusion | flops 196096 | bytes 266240 | tf_op jit(solution)/shard_map/reduce_sum | solution.py:10
  71.7 1.2 %add_convert_fusion = bf16[32,16,128]{2,0,1:T(8,128)(2,1)S(1)} fusion(f32[16,32,128]{2,1,0:T(8,128)} %reduce-scatter.2.cloned.1.call-done, f32[128]{0:T(128)S(1)} %copy-done.5, f32[128]{0:T(128)S(1)} %copy-done.6, f32[32,16]{0,1:T(8,128)S(1)} %add_rsqrt_fusion, f32[32,16]{0,1:T(8,128)S(1)} %broadcast_multiply_fusion), kind=kLoop, calls=%fused_computation.31 | loop fusion | flops 327680 | bytes 398336 | tf_op jit(solution)/shard_map/convert_element_type | solution.py:47
  72.9 0.8 %fusion.3 = bf16[32,16,128]{2,1,0:T(8,128)(2,1)} fusion(f32[32,16,128]{2,1,0:T(8,128)S(1)} %fusion.2, bf16[32,16,128]{2,0,1:T(8,128)(2,1)S(1)} %add_convert_fusion, bf16[128,128]{1,0:T(8,128)(2,1)S(1)} %copy-done.2), kind=kOutput, calls=%fused_computation.6 | convolution fusion | flops 16908288 | bytes 557056 | tf_op jit(solution)/shard_map/rwh,hc->rwc/dot_general | solution.py:51
  (23 shorter events, 0.1 us)
Async XLA Ops:
  6.5 3.3 %copy-start = (bf16[128,512]{1,0:T(8,128)(2,1)S(1)}, bf16[128,512]{1,0:T(8,128)(2,1)}, u32[]{:S(2)}) copy-start(bf16[128,512]{1,0:T(8,128)(2,1)} %param.13) | copy-start | bytes 393220
  29.3 22.6 %all-to-all-start = ((bf16[128,16,128]{2,1,0:T(8,128)(2,1)}), bf16[128,16,128]{2,1,0:T(8,128)(2,1)S(1)}, u32[]{:S(2)}, u32[]{:S(2)}) async-start(bf16[128,16,128]{2,1,0:T(8,128)(2,1)} %all_gather.7), calls=%async_computation | async-start | bytes 1048576 | tf_op jit(solution)/shard_map/all_to_all | solution.py:39
  33.1 36.3 %reduce-scatter.2.cloned.1.call-start = ((), (), s32[]{:S(2)}) async-start(), calls=%async_computation.2 | async-start | bytes 786432 | tf_op jit(solution)/shard_map/reduce_scatter | solution.py:40
  57.3 3.8 %copy-start.1 = (bf16[32,16,128]{2,1,0:T(8,128)(2,1)S(1)}, bf16[32,16,128]{2,1,0:T(8,128)(2,1)}, u32[]{:S(2)}) copy-start(bf16[32,16,128]{2,1,0:T(8,128)(2,1)} %param.9) | copy-start | bytes 393220
  57.3 3.8 %copy-start.3 = (f32[128]{0:T(128)S(1)}, f32[128]{0:T(128)}, u32[]{:S(2)}) copy-start(f32[128]{0:T(128)} %param.12) | copy-start | bytes 1540
  57.3 3.8 %copy-start.4 = (f32[128]{0:T(128)S(1)}, f32[128]{0:T(128)}, u32[]{:S(2)}) copy-start(f32[128]{0:T(128)} %param.11) | copy-start | bytes 1540
  57.3 3.8 %copy-start.7 = (bf16[128,128]{1,0:T(8,128)(2,1)S(1)}, bf16[128,128]{1,0:T(8,128)(2,1)}, u32[]{:S(2)}) copy-start(bf16[128,128]{1,0:T(8,128)(2,1)} %param.14) | copy-start | bytes 98308
  57.3 14.4 %copy-start.5 = (f32[128]{0:T(128)S(1)}, f32[128]{0:T(128)}, u32[]{:S(2)}) copy-start(f32[128]{0:T(128)} %param.16) | copy-start | bytes 1540
  57.4 14.4 %copy-start.6 = (f32[128]{0:T(128)S(1)}, f32[128]{0:T(128)}, u32[]{:S(2)}) copy-start(f32[128]{0:T(128)} %param.15) | copy-start | bytes 1540
  61.1 11.8 %copy-start.2 = (bf16[128,128]{1,0:T(8,128)(2,1)S(1)}, bf16[128,128]{1,0:T(8,128)(2,1)}, u32[]{:S(2)}) copy-start(bf16[128,128]{1,0:T(8,128)(2,1)} %param.17) | copy-start | bytes 98308
Sparse Core Ops, SparseCore 0:
  61.2 8.1 reduce-scatter.1
where the time goes:
time: 81.1 us; the launch traced here: 80.6 us
  blocking collectives  33.6 us (41%)
  between operations  13.6 us (17%)
  local copies, waits for them, and re-layouts  10.6 us (13%)
  waiting for transfers between devices  7.94 us (10%)
  other arithmetic  6.58 us (8%)
  matrix products  4.53 us (6%)
  starting transfers between devices  3.72 us (5%)
    all_gather x1, blocking collectives, on_device(): every_row = lax.all_gather(own_right, 'gx', axis=0, tiled=True)  18 us
    all_gather x1, blocking collectives, on_device(): lax.all_gather(left_side, 'gy', axis=1, tiled=True)  15.6 us
    reduce_scatter x1, waiting for transfers between devices, on_device(): lax.psum_scatter(jnp.einsum('jkc,ikc->jic', row_panel, left_slab, preferr...  7.92 us
    all_to_all x1, starting transfers between devices, on_device(): lax.all_to_all(every_row, 'gy', split_axis=0, concat_axis=1, tiled=True)  3.72 us
    transpose x1, local copies, waits for them, and re-layouts, on_device(): jnp.einsum('jkc,ikc->jic', row_panel, left_slab, preferred_element_type=j...  3.7 us
    all_to_all x2, local copies, waits for them, and re-layouts, on_device(): lax.all_to_all(every_row, 'gy', split_axis=0, concat_axis=1, tiled=True)  3.31 us
    all_gather x1, local copies, waits for them, and re-layouts, on_device(): lax.all_gather(left_side, 'gy', axis=1, tiled=True)  3.21 us
    reduce_sum x2, other arithmetic, normalize(): variance = jnp.mean(centered * centered, axis=-1, keepdims=True)  2.36 us
  transfers between devices with their start and end apart: 2, of which 1 were waited for; matrix products, arithmetic and copies ran while one was open for 4% of the time, Pallas kernels for 0%

commit v1 on v0

--- a/solution.py
+++ b/solution.py
@@ -2,6 +2,11 @@
 import jax.numpy as jnp
 from jax import lax
 from jax.sharding import PartitionSpec as P
+
+
+def all_parts(x, axis, d):
+    blocks = lax.all_gather(x, axis)
+    return jnp.concatenate(blocks, axis=d)
 
 
 def normalize(values, gain, bias):
@@ -32,7 +37,7 @@
     mask_value = pair_mask.astype(jnp.float32)[:, :, None]
     normed, left_side, own_right = project(pair, mask_value, in_gain, in_bias, proj_weight)
     left_slab, right_slab = (
-        lax.all_gather(left_side, "gy", axis=1, tiled=True),
+        all_parts(left_side, "gy", 1),
         lax.all_gather(own_right, "gy", axis=1, tiled=True),
     )
     every_row = lax.all_gather(own_right, "gx", axis=0, tiled=True)

time: 81.1 us -> 74.8 us (0.922)
  local copies, waits for them, and re-layouts: 10.6 us -> 6.89 us
  blocking collectives: 33.6 us -> 31.7 us
    all_gather x1 -> x0, local copies, waits for them, and re-layouts: 3.21 us -> none  [on_device(): lax.all_gather(left_side, 'gy', axis=1, tiled=True)]
    all_gather x1, blocking collectives: 15.6 us -> 13.6 us  [all_parts(): blocks = lax.all_gather(x, axis)]
    reshape x0 -> x2, local copies, waits for them, and re-layouts: none -> 1.68 us  [all_parts(): return jnp.concatenate(blocks, axis=d)]
    transpose x1, local copies, waits for them, and re-layouts: 3.7 us -> 2.21 us  [on_device(): jnp.einsum('jkc,ikc->jic', row_panel, left_slab, preferred_element_type=j...]
  transfers between devices with their start and end apart: 2 -> 2, of which waited for: 1 -> 1; matrix products, arithmetic and copies ran while one was open for 4% -> 3% of each run, Pallas kernels for 0% -> 0%
where the time goes in v1:
time: 74.8 us; the launch traced here: 74.4 us
  blocking collectives  31.7 us (42%)
  between operations  13.6 us (18%)
  waiting for transfers between devices  7.63 us (10%)
  local copies, waits for them, and re-layouts  6.89 us (9%)
  other arithmetic  6.58 us (9%)
  matrix products  4.34 us (6%)
  starting transfers between devices  3.72 us (5%)
    all_gather x1, blocking collectives, on_device(): every_row = lax.all_gather(own_right, 'gx', axis=0, tiled=True)  18 us
    all_gather x1, blocking collectives, all_parts(): blocks = lax.all_gather(x, axis)  13.6 us
    reduce_scatter x1, waiting for transfers between devices, on_device(): lax.psum_scatter(jnp.einsum('jkc,ikc->jic', row_panel, left_slab, preferr...  7.61 us
    all_to_all x1, starting transfers between devices, on_device(): lax.all_to_all(every_row, 'gy', split_axis=0, concat_axis=1, tiled=True)  3.72 us
    all_to_all x2, local copies, waits for them, and re-layouts, on_device(): lax.all_to_all(every_row, 'gy', split_axis=0, concat_axis=1, tiled=True)  2.59 us
    reduce_sum x2, other arithmetic, normalize(): variance = jnp.mean(centered * centered, axis=-1, keepdims=True)  2.36 us
    transpose x1, local copies, waits for them, and re-layouts, on_device(): jnp.einsum('jkc,ikc->jic', row_panel, left_slab, preferred_element_type=j...  2.21 us
    reduce_sum x2, other arithmetic, normalize(): average = jnp.mean(values, axis=-1, keepdims=True)  2.16 us
  transfers between devices with their start and end apart: 2, of which 1 were waited for; matrix products, arithmetic and copies ran while one was open for 3% of the time, Pallas kernels for 0%

profile of v1, /device:TPU:0, one launch (start us, length us, event | category | flops | bytes accessed | tf_op | source)
XLA Modules:
  0.0 74.4 jit_solution(11856309138088779389)
XLA Ops:
  6.5 1.1 %convert_reduce_fusion = f32[32,16]{1,0:T(8,128)S(1)} fusion(bf16[32,16,128]{2,1,0:T(8,128)(2,1)} %param.9), kind=kLoop, calls=%fused_computation.8 | loop fusion | flops 130560 | bytes 133120 | tf_op jit(solution)/shard_map/reduce_sum | solution.py:13
  7.6 0.1 copy.56
  7.7 0.1 copy.57
  7.8 1.1 %fusion.6 = f32[32,16]{1,0:T(8,128)S(1)} fusion(bf16[32,16,128]{2,1,0:T(8,128)(2,1)} %param.9, f32[32,16]{1,0:T(8,128)S(1)} %copy.57), kind=kLoop, calls=%fused_computation.11 | loop fusion | flops 261632 | bytes 135168 | tf_op jit(solution)/shard_map/reduce_sum | solution.py:15
  8.9 0.1 copy.58
  9.0 0.1 copy.59
  9.1 0.7 convert_element_type.23
  9.8 0.1 copy.60
  9.9 1.3 %fusion.20 = f32[32,16,512]{2,1,0:T(8,128)S(1)} fusion(bf16[128,512]{1,0:T(8,128)(2,1)S(1)} %copy-done, bf16[32,16,128]{2,1,0:T(8,128)(2,1)} %param.9, f32[128]{0:T(128)} %param.12, f32[128]{0:T(128)} %param.11, f32[32,16]{1,0:T(8,128)S(1)} %copy.59, f32[32,16]{1,0:T(8,128)S(1)} %copy.57), kind=kOutput, calls=%fused_computation.33 | convolution fusion | flops 67502080 | bytes 1315840 | tf_op jit(solution)/shard_map/rwc,cd->rwd/dot_general | solution.py:22
  11.2 0.2 fusion.11
  11.3 18.0 %all_gather.11 = bf16[128,16,128]{2,1,0:T(8,128)(2,1)} all-gather(bf16[32,16,128]{2,1,0:T(8,128)(2,1)S(1)} %get-tuple-element.5), channel_id=1, replica_groups=mesh['gx'=4,'gy'=4,'gz'=2] {'gx'}, dimensions={0}, use_global_device_ids=true | all-gather | bytes 655360 | tf_op jit(solution)/shard_map/all_gather | solution.py:43
  29.3 3.7 %all-to-all-start = ((bf16[128,16,128]{2,1,0:T(8,128)(2,1)}), bf16[128,16,128]{2,1,0:T(8,128)(2,1)S(1)}, u32[]{:S(2)}, u32[]{:S(2)}) async-start(bf16[128,16,128]{2,1,0:T(8,128)(2,1)} %all_gather.11), calls=%async_computation | async-start | bytes 1048576 | tf_op jit(solution)/shard_map/all_to_all | solution.py:44
  33.1 13.6 %all-gather = bf16[128,16,128]{2,1,0:T(8,128)(2,1)S(1)} all-gather(bf16[32,16,128]{2,1,0:T(8,128)(2,1)S(1)} %get-tuple-element.6), channel_id=2, replica_groups=mesh['gx'=4,'gy'=4,'gz'=2] {'gy'}, dimensions={0}, use_global_device_ids=true | all-gather | bytes 655360 | tf_op jit(solution)/shard_map/all_gather | solution.py:8
  46.7 0.1 copy.61
  46.8 1.6 %copy.63 = bf16[32,64,128]{1,0,2:T(8,128)(2,1)S(1)} copy(bf16[32,64,128]{2,1,0:T(8,128)(2,1)S(1)} %bitcast.28) | data formatting | bytes 1048576 | tf_op jit(solution)/shard_map/reshape | solution.py:9
  48.5 2.5 %copy.64 = bf16[32,64,128]{1,0,2:T(8,128)(2,1)} copy(bf16[32,64,128]{2,1,0:T(8,128)(2,1)S(1)} %bitcast.29) | data formatting | bytes 1048576 | tf_op jit(solution)/shard_map/all_to_all | solution.py:44
  51.0 1.9 %convolution_bitcast_fusion = f32[32,32,128]{0,1,2:T(8,128)S(1)} fusion(bf16[32,64,128]{1,0,2:T(8,128)(2,1)S(1)} %copy.63, bf16[32,64,128]{1,0,2:T(8,128)(2,1)} %copy.64), kind=kOutput, calls=%fused_computation | convolution fusion | flops 16777216 | bytes 1572864 | tf_op jit(solution)/shard_map/jkc,ikc->jic/dot_general | solution.py:46
  53.0 2.2 %copy.65 = f32[32,32,128]{2,1,0:T(8,128)} copy(f32[32,32,128]{0,1,2:T(8,128)S(1)} %convolution_bitcast_fusion) | data formatting | bytes 1048576 | tf_op jit(solution)/shard_map/jkc,ikc->jic/transpose | solution.py:46
  55.3 0.3 fusion.2
  55.6 7.6 %reduce-scatter.2.cloned.1.call-done = f32[16,32,128]{2,1,0:T(8,128)} async-done(((f32[32,32,128]{2,1,0:T(8,128)}), f32[16,32,128]{2,1,0:T(8,128)}) %reduce-scatter.2.cloned.1.call-update) | async-done | bytes 262160 | tf_op jit(solution)/shard_map/reduce_scatter | solution.py:45
  63.2 1.1 %bitcast_reduce_fusion = f32[32,16]{0,1:T(8,128)S(1)} fusion(f32[16,32,128]{2,1,0:T(8,128)} %reduce-scatter.2.cloned.1.call-done), kind=kLoop, calls=%fused_computation.30 | loop fusion | flops 65024 | bytes 264192 | tf_op jit(solution)/shard_map/reduce_sum | solution.py:13
  64.3 1.2 %multiply_reduce_fusion = f32[32,16]{0,1:T(8,128)S(1)} fusion(f32[16,32,128]{2,1,0:T(8,128)} %reduce-scatter.2.cloned.1.call-done, f32[32,16]{0,1:T(8,128)S(1)} %broadcast_multiply_fusion), kind=kLoop, calls=%fused_computation.32 | loop fusion | flops 196096 | bytes 266240 | tf_op jit(solution)/shard_map/reduce_sum | solution.py:15
  65.6 1.2 %add_convert_fusion = bf16[32,16,128]{2,0,1:T(8,128)(2,1)S(1)} fusion(f32[16,32,128]{2,1,0:T(8,128)} %reduce-scatter.2.cloned.1.call-done, f32[128]{0:T(128)S(1)} %copy-done.5, f32[128]{0:T(128)S(1)} %copy-done.6, f32[32,16]{0,1:T(8,128)S(1)} %add_rsqrt_fusion, f32[32,16]{0,1:T(8,128)S(1)} %broadcast_multiply_fusion), kind=kLoop, calls=%fused_computation.31 | loop fusion | flops 327680 | bytes 398336 | tf_op jit(solution)/shard_map/convert_element_type | solution.py:52
  66.7 0.8 %fusion.3 = bf16[32,16,128]{2,1,0:T(8,128)(2,1)} fusion(f32[32,16,128]{2,1,0:T(8,128)S(1)} %fusion.2, bf16[32,16,128]{2,0,1:T(8,128)(2,1)S(1)} %add_convert_fusion, bf16[128,128]{1,0:T(8,128)(2,1)S(1)} %copy-done.2), kind=kOutput, calls=%fused_computation.6 | convolution fusion | flops 16908288 | bytes 557056 | tf_op jit(solution)/shard_map/rwh,hc->rwc/dot_general | solution.py:56
  (24 shorter events, 0.1 us)
Async XLA Ops:
  6.5 3.3 %copy-start = (bf16[128,512]{1,0:T(8,128)(2,1)S(1)}, bf16[128,512]{1,0:T(8,128)(2,1)}, u32[]{:S(2)}) copy-start(bf16[128,512]{1,0:T(8,128)(2,1)} %param.13) | copy-start | bytes 393220
  29.3 19.1 %all-to-all-start = ((bf16[128,16,128]{2,1,0:T(8,128)(2,1)}), bf16[128,16,128]{2,1,0:T(8,128)(2,1)S(1)}, u32[]{:S(2)}, u32[]{:S(2)}) async-start(bf16[128,16,128]{2,1,0:T(8,128)(2,1)} %all_gather.11), calls=%async_computation | async-start | bytes 1048576 | tf_op jit(solution)/shard_map/all_to_all | solution.py:44
  33.1 30.1 %reduce-scatter.2.cloned.1.call-start = ((), (), s32[]{:S(2)}) async-start(), calls=%async_computation.2 | async-start | bytes 786432 | tf_op jit(solution)/shard_map/reduce_scatter | solution.py:45
  52.9 2.3 %copy-start.1 = (bf16[32,16,128]{2,1,0:T(8,128)(2,1)S(1)}, bf16[32,16,128]{2,1,0:T(8,128)(2,1)}, u32[]{:S(2)}) copy-start(bf16[32,16,128]{2,1,0:T(8,128)(2,1)} %param.9) | copy-start | bytes 393220
  52.9 2.3 %copy-start.3 = (f32[128]{0:T(128)S(1)}, f32[128]{0:T(128)}, u32[]{:S(2)}) copy-start(f32[128]{0:T(128)} %param.12) | copy-start | bytes 1540
  52.9 2.3 %copy-start.4 = (f32[128]{0:T(128)S(1)}, f32[128]{0:T(128)}, u32[]{:S(2)}) copy-start(f32[128]{0:T(128)} %param.11) | copy-start | bytes 1540
  52.9 2.3 %copy-start.7 = (bf16[128,128]{1,0:T(8,128)(2,1)S(1)}, bf16[128,128]{1,0:T(8,128)(2,1)}, u32[]{:S(2)}) copy-start(bf16[128,128]{1,0:T(8,128)(2,1)} %param.14) | copy-start | bytes 98308
  52.9 12.6 %copy-start.5 = (f32[128]{0:T(128)S(1)}, f32[128]{0:T(128)}, u32[]{:S(2)}) copy-start(f32[128]{0:T(128)} %param.16) | copy-start | bytes 1540
  53.0 12.6 %copy-start.6 = (f32[128]{0:T(128)S(1)}, f32[128]{0:T(128)}, u32[]{:S(2)}) copy-start(f32[128]{0:T(128)} %param.15) | copy-start | bytes 1540
  55.2 11.5 %copy-start.2 = (bf16[128,128]{1,0:T(8,128)(2,1)S(1)}, bf16[128,128]{1,0:T(8,128)(2,1)}, u32[]{:S(2)}) copy-start(bf16[128,128]{1,0:T(8,128)(2,1)} %param.17) | copy-start | bytes 98308
Sparse Core Ops, SparseCore 0:
  55.3 7.8 reduce-scatter.1
